TPU v7x, 32 devices: a whole 2x2x4 slice. The times are simulated.
32 devices in a mesh: traj: 4 (over y, x), grid: 8 (over z, core).
Axes of the slice: x: 2, y: 2, z: 4, core: 2. Of those that a mesh axis runs over, the one named last changes fastest.
Arguments:
- psi_modes: float32 [4, 2, 256, 256, 256], P('traj', None, None, 'grid'), may hold values from -6 to 6
- noise: float32 [4, 2, 256, 256, 256], P('traj', None, 'grid'), may hold values from -6 to 6
- mask: int32 [256, 256, 256], P(None, 'grid'), may hold values from 0 to 1, as said below
Outputs:
- psi_next: float32 [4, 2, 256, 256, 256], P('traj', None, None, 'grid')
- momentum_hist: float32 [128], replicated
Inputs may be any that keep to these rules, and one draw needn't show every extreme that they name: mask is 0 at every mode whose signed third index has magnitude 256/4 or more, and 1 at some mode whose signed third index has magnitude 256/4 - 1.
All inputs are finite; a program needn't handle non-finite values.
Results may differ from a plain program's by a relative error of at most 0.00023.
Values sent between devices are 32-bit elements; how exact they have to be, the bound alone decides.
A program may use at most 192 MiB of HBM per device.

v0:
```python
import jax
import jax.numpy as jnp
from jax import lax
from jax.sharding import PartitionSpec as P

SHELLS = 128
time_step = 1.0
damping = 0.05
coupling = 10.0
chem_potential = 1.0
noise_amp = 0.1
trap_strength = 8.0
max_chunks = 4


def signed_of(index, count):
    return jnp.where(index < count // 2, index, index - count)


def dft_table(out_index, in_index, count, sign):
    phase = (out_index[:, None] * in_index[None, :] % count).astype(jnp.float32) * (
        2.0 * jnp.pi / count
    )
    scale = 1.0 / jnp.sqrt(jnp.float32(count))
    return (jnp.cos(phase) * scale, sign * jnp.sin(phase) * scale)


def axis_factor(modes, count):
    wave = modes.astype(jnp.float32) * (2.0 * jnp.pi / count)
    theta = 0.25 * time_step * wave * wave
    size = jnp.exp(-damping * theta)
    return (size * jnp.cos(theta), -size * jnp.sin(theta))


def scaled(table, factor, dim):
    real, imag = factor
    if dim == 0:
        real, imag = (real[:, None], imag[:, None])
    else:
        real, imag = (real[None, :], imag[None, :])
    return (table[0] * real - table[1] * imag, table[0] * imag + table[1] * real)


def block_table(table):
    real, imag = table
    top = jnp.stack([real, -imag], axis=1)
    bottom = jnp.stack([imag, real], axis=1)
    return jnp.stack([top, bottom], axis=0)


def contract(pattern, table, values):
    return jnp.einsum(pattern, table, values, precision=lax.Precision.HIGH)


def cos_sin(angle):
    turns = jnp.round(angle * (2.0 / jnp.pi))
    rest = angle - turns * 1.5703125
    rest = rest - turns * 0.0004837512969970703
    rest = rest - turns * 7.549789954891882e-08
    sq = rest * rest
    sine = rest + rest * sq * (-0.16666654611 + sq * (0.0083321608736 + sq * -0.00019515295891))
    cosine = 1.0 + sq * (
        -0.5
        + sq * (0.04166664568298827 + sq * (-0.001388731625493765 + sq * 2.443315711809948e-05))
    )
    quadrant = turns.astype(jnp.int32)
    odd = quadrant & 1 != 0
    cos_out = jnp.where(odd, sine, cosine)
    sin_out = jnp.where(odd, cosine, sine)
    cos_out = jnp.where(quadrant + 1 & 2 != 0, -cos_out, cos_out)
    sin_out = jnp.where(quadrant & 2 != 0, -sin_out, sin_out)
    return (cos_out, sin_out)


def shell_sums(occupation, modes_x, modes_y, modes_z, limit):
    base = (modes_x[:, None] ** 2 + modes_y[None, :] ** 2) * SHELLS
    row_shell = jnp.minimum(base // limit, SHELLS - 1).reshape(-1)
    row_rest = (base % limit).reshape(-1)
    col = modes_z**2 * SHELLS
    col_shell = col // limit
    col_rest = col % limit
    flat = occupation.reshape(row_rest.shape[0], -1)
    carry = row_rest[:, None] + col_rest[None, :] >= limit
    zero = jnp.float32(0.0)
    both = jnp.concatenate([jnp.where(carry, zero, flat), jnp.where(carry, flat, zero)], axis=-1)
    shell_ids = jnp.arange(SHELLS, dtype=jnp.int32)
    hits = (row_shell[None, :] == shell_ids[:, None]).astype(jnp.float32)
    sums = jnp.einsum("sr,rc->sc", hits, both, precision=lax.Precision.HIGHEST)
    offset = jnp.concatenate([col_shell, col_shell + 1])
    shell = jnp.minimum(shell_ids[:, None] + offset[None, :], SHELLS - 1)
    picked = jnp.where(shell[None] == shell_ids[:, None, None], sums[None], zero)
    return jnp.sum(picked, axis=(1, 2))


def shards(psi_modes, noise, mask):
    grid_rank = lax.axis_index("grid")
    ranks = lax.axis_size("grid")
    extent_x = mask.shape[0]
    extent_y = noise.shape[3]
    extent_z = mask.shape[2]
    rows_local = mask.shape[1]
    planes_local = noise.shape[2]
    quarter = extent_z // 4
    chunks = max_chunks
    while planes_local % chunks:
        chunks -= 1
    depth = planes_local // chunks

    def select_cols(values):
        return jnp.concatenate([values[..., :quarter], values[..., extent_z - quarter :]], axis=-1)

    index_x, index_y, all_cols = lax.optimization_barrier(
        tuple((jnp.arange(extent, dtype=jnp.int32) for extent in (extent_x, extent_y, extent_z)))
    )
    column_ids = select_cols(all_cols)
    modes_x = signed_of(index_x, extent_x)
    modes_y_all = signed_of(index_y, extent_y)
    modes_y = signed_of(grid_rank * rows_local + jnp.arange(rows_local, dtype=jnp.int32), extent_y)
    modes_z = signed_of(column_ids, extent_z)
    fac_x = axis_factor(modes_x, extent_x)
    fac_y = axis_factor(modes_y_all, extent_y)
    fac_z = axis_factor(modes_z, extent_z)
    inverse_x = block_table(scaled(dft_table(index_x, index_x, extent_x, 1.0), fac_x, 1))
    inverse_y = block_table(scaled(dft_table(index_y, index_y, extent_y, 1.0), fac_y, 1))
    inverse_z = block_table(scaled(dft_table(all_cols, column_ids, extent_z, 1.0), fac_z, 1))
    forward_x = block_table(scaled(dft_table(index_x, index_x, extent_x, -1.0), fac_x, 0))
    forward_y = block_table(scaled(dft_table(index_y, index_y, extent_y, -1.0), fac_y, 0))
    forward_z = block_table(scaled(dft_table(column_ids, all_cols, extent_z, -1.0), fac_z, 0))
    inverse_x = inverse_x.reshape(2, ranks, chunks, depth, 2, extent_x)
    inverse_y = inverse_y.reshape(2, extent_y, 2, ranks, rows_local)
    forward_y = forward_y.reshape(2, ranks, rows_local, 2, extent_y)
    forward_x = forward_x.reshape(2, extent_x, 2, ranks, chunks, depth)
    kept = select_cols(mask).astype(jnp.float32)
    start = select_cols(psi_modes) * kept
    pos_x = (grid_rank * planes_local + jnp.arange(planes_local, dtype=jnp.int32)).astype(
        jnp.float32
    )
    pos_x = (pos_x + 0.5) / extent_x - 0.5
    pos_y = (index_y.astype(jnp.float32) + 0.5) / extent_y - 0.5
    pos_z = (all_cols.astype(jnp.float32) + 0.5) / extent_z - 0.5

    def exchange(values):
        return lax.all_to_all(values, "grid", split_axis=2, concat_axis=2, tiled=True)

    arrived = [
        exchange(contract("dgpcx,tcxyz->tdgpyz", inverse_x[:, :, chunk], start))
        for chunk in range(chunks)
    ]
    final = None
    for chunk in range(chunks):
        low = chunk * depth
        spaced = contract("ekdsy,tdspyz->tepkz", inverse_y, arrived[chunk])
        field = contract("ekdz,tdpyz->tepyk", inverse_z, spaced)
        field_real, field_imag = (field[:, 0], field[:, 1])
        potential = trap_strength * (
            pos_x[low : low + depth, None, None] ** 2
            + pos_y[None, :, None] ** 2
            + pos_z[None, None, :] ** 2
        )
        density = field_real * field_real + field_imag * field_imag
        energy = potential + coupling * density - chem_potential
        decay = jnp.exp(-damping * energy * time_step)
        cosine, sine = cos_sin(jnp.minimum(energy * time_step, 4096.0))
        evo_real = decay * cosine
        evo_imag = -decay * sine
        kick = noise_amp * noise[:, :, low : low + depth]
        moved = jnp.stack(
            [
                field_real * evo_real - field_imag * evo_imag + kick[:, 0],
                field_real * evo_imag + field_imag * evo_real + kick[:, 1],
            ],
            axis=1,
        )
        partial_fwd = contract("ekdz,tdpyz->tepyk", forward_z, moved)
        partial_fwd = contract("egkdy,tdpyz->tegpkz", forward_y, partial_fwd)
        returned = exchange(partial_fwd)
        piece = contract("ekdsp,tdspyz->tekyz", forward_x[:, :, :, :, chunk], returned)
        final = piece if final is None else final + piece
    out = final * kept
    occupation = jnp.sum(out * out, axis=(0, 1))
    local_hist = shell_sums(occupation, modes_x, modes_y, modes_z, 2 * quarter * quarter)
    total_hist = lax.psum(local_hist, ("traj", "grid"))
    traj_count = psi_modes.shape[0] * lax.axis_size("traj")
    momentum_hist = total_hist * (SHELLS / (traj_count * extent_x * extent_y * extent_z))
    filler = jnp.zeros(out.shape[:-1] + (extent_z - 2 * quarter,), jnp.float32)
    psi_next = jnp.concatenate([out[..., :quarter], filler, out[..., quarter:]], axis=-1)
    return (psi_next, momentum_hist)


def solution(mesh):
    placed = (
        P("traj", None, None, "grid", None),
        P("traj", None, "grid", None, None),
        P(None, "grid", None),
    )
    return jax.shard_map(
        shards,
        mesh=mesh,
        in_specs=placed,
        out_specs=(P("traj", None, None, "grid", None), P()),
        check_vma=False,
    )
```

profile of v0, /device:TPU:10, one launch (start us, length us, event | category | flops | bytes accessed | tf_op | source)
XLA Modules:
  0.0 574.9 jit_solution(2185708760382104908)
XLA Ops:
  0.8 4.9 fusion.186
  5.8 9.4 %slice_bitcast_fusion.1 = (f32[2,256,32,64]{3,2,1,0:T(8,128)S(1)}, f32[2,256,32,64]{3,2,1,0:T(8,128)}) fusion(f32[1,2,256,32,256]{4,3,2,1,0:T(8,128)} %param.3), kind=kLoop, calls=%fused_computation.15 | loop fusion | bytes 16777216 | tf_op jit(solution)/shard_map/concatenate | solution.py:110
  17.5 5.5 fusion
  23.1 7.0 %fusion.104 = f32[1,2,8,8,32,128]{5,3,2,1,4,0:T(8,128)S(1)} fusion(f32[2,256,32,128,1,1]{3,2,1,0,5,4:T(8,128)S(1)} %fusion, f32[2,8,4,8,2,256]{5,3,4,1,0,2:T(8,128)S(1)} %maximum_maximum_fusion), kind=kOutput, calls=%fused_computation.202 | convolution fusion | flops 1610612736 | bytes 10747904 | tf_op jit(solution)/shard_map/dgpcx,tcxyz->tdgpyz/dot_general | solution.py:52
  30.2 1.6 copy.131
  31.7 5.5 all-to-all-start.2
  37.2 9.9 %fusion.101 = f32[1,2,8,8,32,128]{5,3,2,1,4,0:T(8,128)S(1)} fusion(f32[2,256,32,128,1,1]{3,2,1,0,5,4:T(8,128)} %copy-done, f32[2,8,4,8,2,256]{5,3,4,1,0,2:T(8,128)S(1)} %maximum_maximum_fusion), kind=kOutput, calls=%fused_computation.201 | convolution fusion | flops 1610612736 | bytes 10747904 | tf_op jit(solution)/shard_map/dgpcx,tcxyz->tdgpyz/dot_general | solution.py:52
  48.7 34.0 %all-to-all-done.2 = f32[1,2,8,8,32,128]{5,3,1,4,0,2:T(8,128)S(1)} async-done(((f32[1,2,8,8,32,128]{5,3,1,4,0,2:T(8,128)}), f32[1,2,8,8,32,128]{5,3,1,4,0,2:T(8,128)S(1)}, u32[]{:S(2)}, u32[]{:S(2)}) %all-to-all-start.2) | async-done | bytes 2097184 | tf_op jit(solution)/shard_map/all_to_all | solution.py:143
  84.2 8.1 %all-to-all-start = ((f32[1,2,8,8,32,128]{5,3,1,4,0,2:T(8,128)}), f32[1,2,8,8,32,128]{5,3,1,4,0,2:T(8,128)}, u32[]{:S(2)}, u32[]{:S(2)}) async-start(f32[1,2,8,8,32,128]{5,3,1,4,0,2:T(8,128)} %copy.123), calls=%async_computation | async-start | bytes 4194304 | tf_op jit(solution)/shard_map/all_to_all | solution.py:143
  92.2 9.9 %fusion.110 = f32[1,2,8,8,32,128]{5,3,2,1,4,0:T(8,128)S(1)} fusion(f32[2,256,32,128,1,1]{3,2,1,0,5,4:T(8,128)} %copy-done, f32[2,8,4,8,2,256]{5,3,4,1,0,2:T(8,128)S(1)} %maximum_maximum_fusion), kind=kOutput, calls=%fused_computation.204 | convolution fusion | flops 1610612736 | bytes 10747904 | tf_op jit(solution)/shard_map/dgpcx,tcxyz->tdgpyz/dot_general | solution.py:52
  103.9 11.4 %fusion.107 = f32[1,2,8,8,32,128]{5,3,2,1,4,0:T(8,128)} fusion(f32[2,256,32,128,1,1]{3,2,1,0,5,4:T(8,128)} %copy-done, f32[2,8,4,8,2,256]{5,3,4,1,0,2:T(8,128)S(1)} %maximum_maximum_fusion), kind=kOutput, calls=%fused_computation.203 | convolution fusion | flops 1610612736 | bytes 10747904 | tf_op jit(solution)/shard_map/dgpcx,tcxyz->tdgpyz/dot_general | solution.py:52
  115.3 22.1 %all-to-all-done = f32[1,2,8,8,32,128]{5,3,1,4,0,2:T(8,128)} async-done(((f32[1,2,8,8,32,128]{5,3,1,4,0,2:T(8,128)}), f32[1,2,8,8,32,128]{5,3,1,4,0,2:T(8,128)}, u32[]{:S(2)}, u32[]{:S(2)}) %all-to-all-start) | async-done | bytes 2097184 | tf_op jit(solution)/shard_map/all_to_all | solution.py:143
  137.4 7.1 %all-to-all-start.6 = ((f32[1,2,8,8,32,128]{5,3,1,4,0,2:T(8,128)}), f32[1,2,8,8,32,128]{5,3,1,4,0,2:T(8,128)S(1)}, u32[]{:S(2)}, u32[]{:S(2)}) async-start(f32[1,2,8,8,32,128]{5,3,1,4,0,2:T(8,128)} %copy.145), calls=%async_computation.6 | async-start | bytes 4194304 | tf_op jit(solution)/shard_map/all_to_all | solution.py:143
  144.9 3.2 copy.138
  151.2 1.9 fusion.155
  154.2 10.1 %fusion.184 = (f32[1,2,8,256,256]{4,3,2,1,0:T(8,128)}, f32[1,2,8,256,256]{4,3,2,1,0:T(8,128)}, f32[1,2,8,256,256]{4,3,2,1,0:T(8,128)S(1)}, f32[1,2,8,256,256]{4,3,2,1,0:T(8,128)S(1)}) fusion(f32[1,2,32,256,256]{4,3,2,1,0:T(8,128)} %param.4), kind=kLoop, calls=%fused_computation.386 | loop fusion | bytes 33554432 | tf_op jit(solution)/shard_map/slice | solution.py:166
  164.4 4.0 copy_multiply_fusion.2
  168.4 21.7 %all-to-all-done.6 = f32[1,2,8,8,32,128]{5,3,1,4,0,2:T(8,128)S(1)} async-done(((f32[1,2,8,8,32,128]{5,3,1,4,0,2:T(8,128)}), f32[1,2,8,8,32,128]{5,3,1,4,0,2:T(8,128)S(1)}, u32[]{:S(2)}, u32[]{:S(2)}) %all-to-all-start.6) | async-done | bytes 2097184 | tf_op jit(solution)/shard_map/all_to_all | solution.py:143
  190.1 7.7 %all-to-all-start.4 = ((f32[1,2,8,8,32,128]{5,3,1,4,0,2:T(8,128)}), f32[1,2,8,8,32,128]{5,3,1,4,0,2:T(8,128)}, u32[]{:S(2)}, u32[]{:S(2)}) async-start(f32[1,2,8,8,32,128]{5,3,1,4,0,2:T(8,128)} %copy.138), calls=%async_computation.4 | async-start | bytes 4194304 | tf_op jit(solution)/shard_map/all_to_all | solution.py:143
  197.8 4.1 fusion.84
  201.9 4.1 fusion.90
  206.0 3.6 convolution_bitcast_fusion.2
  209.6 3.6 convolution_bitcast_fusion.3
  213.3 10.2 %slice_add_fusion.7 = (f32[1,1,8,256,256]{4,3,1,2,0:T(8,128)S(1)}, f32[1,1,8,256,256]{4,3,1,2,0:T(8,128)S(1)}, f32[1,1,8,256,256]{4,3,1,2,0:T(8,128)}, f32[1,1,8,256,256]{4,3,1,2,0:T(8,128)}) fusion(f32[1,2,8,256,256]{4,3,1,2,0:T(8,128)S(1)} %copy-done.5, f32[1,2,8,256,256]{4,3,1,2,0:T(8,128)S(1)} %convolution_bitcast_fusion.3, ...), kind=kLoop, calls=%fused_computation.136 | loop fusion | flops 61865984 | bytes 25183232 | tf_op jit(solution)/shard_map/add | solution.py:169
  223.5 1.9 fusion.13
  225.4 1.9 fusion.113
  227.2 1.6 copy.127
  228.8 14.5 %all-to-all-done.4 = f32[1,2,8,8,32,128]{5,3,1,4,0,2:T(8,128)} async-done(((f32[1,2,8,8,32,128]{5,3,1,4,0,2:T(8,128)}), f32[1,2,8,8,32,128]{5,3,1,4,0,2:T(8,128)}, u32[]{:S(2)}, u32[]{:S(2)}) %all-to-all-start.4) | async-done | bytes 2097184 | tf_op jit(solution)/shard_map/all_to_all | solution.py:143
  243.4 7.8 %all-to-all-start.1 = ((f32[1,2,8,8,32,128]{5,4,1,3,0,2:T(8,128)}), f32[1,2,8,8,32,128]{5,4,1,3,0,2:T(8,128)}, u32[]{:S(2)}, u32[]{:S(2)}) async-start(f32[1,2,8,8,32,128]{5,4,1,3,0,2:T(8,128)} %copy.127), calls=%async_computation.1 | async-start | bytes 4194304 | tf_op jit(solution)/shard_map/all_to_all | solution.py:143
  251.2 8.0 %copy_multiply_fusion = (f32[1,2,8,256,256]{4,3,1,2,0:T(8,128)}, f32[1,2,8,256,256]{4,3,1,2,0:T(8,128)}) fusion(f32[1,2,8,256,256]{4,3,2,1,0:T(8,128)} %get-tuple-element.22, f32[1,2,8,256,256]{4,3,2,1,0:T(8,128)} %get-tuple-element.23), kind=kLoop, calls=%fused_computation.41 | loop fusion | flops 2097152 | bytes 16777216 | tf_op jit(solution)/shard_map/mul | solution.py:166
  259.3 1.9 fusion.16
  261.2 1.9 fusion.116
  263.0 1.6 copy.135
  264.6 32.2 %all-to-all-done.1 = f32[1,2,8,8,32,128]{5,4,1,3,0,2:T(8,128)} async-done(((f32[1,2,8,8,32,128]{5,4,1,3,0,2:T(8,128)}), f32[1,2,8,8,32,128]{5,4,1,3,0,2:T(8,128)}, u32[]{:S(2)}, u32[]{:S(2)}) %all-to-all-start.1) | async-done | bytes 2097184 | tf_op jit(solution)/shard_map/all_to_all | solution.py:143
  296.8 8.0 %all-to-all-start.3 = ((f32[1,2,8,8,32,128]{5,4,1,3,0,2:T(8,128)}), f32[1,2,8,8,32,128]{5,4,1,3,0,2:T(8,128)}, u32[]{:S(2)}, u32[]{:S(2)}) async-start(f32[1,2,8,8,32,128]{5,4,1,3,0,2:T(8,128)} %copy.135), calls=%async_computation.3 | async-start | bytes 4194304 | tf_op jit(solution)/shard_map/all_to_all | solution.py:143
  304.8 3.5 fusion.72
  308.3 4.1 fusion.78
  312.4 3.6 convolution_bitcast_fusion
  316.1 3.6 convolution_bitcast_fusion.1
  319.7 10.0 %slice_add_fusion.1 = (f32[1,1,8,256,256]{4,3,1,2,0:T(8,128)}, f32[1,1,8,256,256]{4,3,1,2,0:T(8,128)}, f32[1,1,8,256,256]{4,3,1,2,0:T(8,128)S(1)}, f32[1,1,8,256,256]{4,3,1,2,0:T(8,128)S(1)}) fusion(f32[1,2,8,256,256]{4,3,1,2,0:T(8,128)S(1)} %copy-done.2, f32[1,2,8,256,256]{4,3,1,2,0:T(8,128)S(1)} %convolution_bitcast_fusion, ...), kind=kLoop, calls=%fused_computation.130 | loop fusion | flops 61865984 | bytes 25183232 | tf_op jit(solution)/shard_map/add | solution.py:169
  329.7 1.9 fusion.19
  331.6 1.9 fusion.119
  335.0 15.4 %all-to-all-done.3 = f32[1,2,8,8,32,128]{5,4,1,3,0,2:T(8,128)} async-done(((f32[1,2,8,8,32,128]{5,4,1,3,0,2:T(8,128)}), f32[1,2,8,8,32,128]{5,4,1,3,0,2:T(8,128)}, u32[]{:S(2)}, u32[]{:S(2)}) %all-to-all-start.3) | async-done | bytes 2097184 | tf_op jit(solution)/shard_map/all_to_all | solution.py:143
  350.3 7.1 %all-to-all-start.5 = ((f32[1,2,8,8,32,128]{5,4,1,3,0,2:T(8,128)}), f32[1,2,8,8,32,128]{5,4,1,3,0,2:T(8,128)S(1)}, u32[]{:S(2)}, u32[]{:S(2)}) async-start(f32[1,2,8,8,32,128]{5,4,1,3,0,2:T(8,128)} %copy.142), calls=%async_computation.5 | async-start | bytes 4194304 | tf_op jit(solution)/shard_map/all_to_all | solution.py:143
  357.4 3.7 fusion.22
  361.1 1.9 fusion.122
  363.0 1.6 copy.149
  364.6 38.4 %all-to-all-done.5 = f32[1,2,8,8,32,128]{5,4,1,3,0,2:T(8,128)S(1)} async-done(((f32[1,2,8,8,32,128]{5,4,1,3,0,2:T(8,128)}), f32[1,2,8,8,32,128]{5,4,1,3,0,2:T(8,128)S(1)}, u32[]{:S(2)}, u32[]{:S(2)}) %all-to-all-start.5) | async-done | bytes 2097184 | tf_op jit(solution)/shard_map/all_to_all | solution.py:143
  403.0 8.2 %all-to-all-start.7 = ((f32[1,2,8,8,32,128]{5,4,1,3,0,2:T(8,128)}), f32[1,2,8,8,32,128]{5,4,1,3,0,2:T(8,128)}, u32[]{:S(2)}, u32[]{:S(2)}) async-start(f32[1,2,8,8,32,128]{5,4,1,3,0,2:T(8,128)} %copy.149), calls=%async_computation.7 | async-start | bytes 4194304 | tf_op jit(solution)/shard_map/all_to_all | solution.py:143
  411.3 5.3 copy.151
  418.2 8.8 %fusion.86 = f32[32,128,2,256,1,1]{3,1,5,4,2,0:T(8,128)} fusion(f32[1,2,8,8,32,128]{5,4,1,3,0,2:T(8,128)} %all-to-all-done.1, f32[2,256,2,8,4,8]{1,3,5,2,0,4:T(8,128)S(1)} %maximum_maximum_fusion.1), kind=kOutput, calls=%fused_computation.158 | convolution fusion | flops 1610612736 | bytes 10747904 | tf_op jit(solution)/shard_map/ekdsp,tdspyz->tekyz/dot_general | solution.py:52
  427.0 8.8 %fusion.80 = f32[32,128,2,256,1,1]{3,1,5,4,2,0:T(8,128)} fusion(f32[1,2,8,8,32,128]{5,4,1,3,0,2:T(8,128)} %all-to-all-done.3, f32[2,256,2,8,4,8]{1,3,5,2,0,4:T(8,128)S(1)} %maximum_maximum_fusion.1), kind=kOutput, calls=%fused_computation.152 | convolution fusion | flops 1610612736 | bytes 10747904 | tf_op jit(solution)/shard_map/ekdsp,tdspyz->tekyz/dot_general | solution.py:52
  435.8 6.8 %fusion.74 = f32[32,128,2,256,1,1]{3,1,5,4,2,0:T(8,128)} fusion(f32[1,2,8,8,32,128]{5,4,1,3,0,2:T(8,128)S(1)} %all-to-all-done.5, f32[2,256,2,8,4,8]{1,3,5,2,0,4:T(8,128)S(1)} %maximum_maximum_fusion.1), kind=kOutput, calls=%fused_computation.146 | convolution fusion | flops 1610612736 | bytes 10747904 | tf_op jit(solution)/shard_map/ekdsp,tdspyz->tekyz/dot_general | solution.py:52
  442.6 14.1 %all-to-all-done.7 = f32[1,2,8,8,32,128]{5,4,1,3,0,2:T(8,128)} async-done(((f32[1,2,8,8,32,128]{5,4,1,3,0,2:T(8,128)}), f32[1,2,8,8,32,128]{5,4,1,3,0,2:T(8,128)}, u32[]{:S(2)}, u32[]{:S(2)}) %all-to-all-start.7) | async-done | bytes 2097184 | tf_op jit(solution)/shard_map/all_to_all | solution.py:143
  456.7 18.4 %multiply_reduce_fusion = (f32[256,32,128]{0,2,1:T(8,128)}, f32[1,2,256,32,128]{2,4,1,3,0:T(8,128)}) fusion(f32[256,32,128]{0,2,1:T(8,128)} %copy.151, f32[2,256,2,8,4,8]{1,3,5,2,0,4:T(8,128)S(1)} %maximum_maximum_fusion.1, f32[1,2,8,8,32,128]{5,4,1,3,0,2:T(8,128)} %all-to-all-done.7, f32[32,128,2,256,1,1]{3,1,5,4,2,0:T(8,128)} %fusion.74, ...), kind=kOutput, calls=%fused_computation.13 | convolution fusion | flops 1622147072 | bytes 44302336 | tf_op jit(solution)/shard_map/ekdsp,tdspyz->tekyz/dot_general | solution.py:52
  475.1 5.5 copy.154
  480.5 5.9 %bitcast_select_fusion.1 = (f32[8192,128]{1,0:T(8,128)S(1)}, f32[8192,128]{1,0:T(8,128)S(1)}) fusion(f32[256,32,128]{2,1,0:T(8,128)} %copy.154, s32[128]{0:T(128)S(1)} %and_select_fusion, s32[8192]{0:T(1024)S(1)} %get-tuple-element.47), kind=kLoop, calls=%fused_computation.46 | loop fusion | flops 4194304 | bytes 12616192 | tf_op jit(solution)/shard_map/jit(_where)/select_n | solution.py:85
  486.4 3.4 fusion.1
  489.9 1.9 select_reduce_fusion
  491.8 43.2 %psum.7 = f32[128]{0:T(128)S(1)} all-reduce(f32[128]{0:T(128)S(1)} %select_reduce_fusion), channel_id=1, replica_groups=mesh['traj'=4,'grid'=8] {'traj','grid'}, use_global_device_ids=true, to_apply=%region_2.3 | all-reduce | flops 128 | bytes 1024 | tf_op jit(solution)/shard_map/psum | solution.py:182
  535.5 7.8 %fusion.185 = (f32[1,2,256,32,64]{2,4,1,3,0:T(8,128)}, f32[1,2,256,32,64]{2,4,1,3,0:T(8,128)}) fusion(f32[1,2,256,32,128]{2,4,1,3,0:T(8,128)} %get-tuple-element.89), kind=kLoop, calls=%fused_computation.387 | loop fusion | bytes 16777216 | tf_op jit(solution)/shard_map/slice | solution.py:186
  543.3 9.2 %copy.152 = f32[1,2,256,32,64]{4,3,2,1,0:T(8,128)} copy(f32[1,2,256,32,64]{2,4,1,3,0:T(8,128)} %get-tuple-element.36) | data formatting | bytes 8388608 | tf_op jit(solution)/shard_map/slice | solution.py:186
  552.6 9.2 %copy.153 = f32[1,2,256,32,64]{4,3,2,1,0:T(8,128)} copy(f32[1,2,256,32,64]{2,4,1,3,0:T(8,128)} %get-tuple-element.37) | data formatting | bytes 8388608 | tf_op jit(solution)/shard_map/slice | solution.py:186
  561.7 13.0 %pad_maximum_fusion = f32[1,2,256,32,256]{4,3,2,1,0:T(8,128)} fusion(f32[1,2,256,32,64]{4,3,2,1,0:T(8,128)} %copy.153, f32[1,2,256,32,64]{4,3,2,1,0:T(8,128)} %copy.152, f32[256]{0:T(256)S(1)} %pad.5.clone), kind=kLoop, calls=%fused_computation | loop fusion | flops 8388608 | bytes 25166848 | tf_op jit(solution)/shard_map/concatenate | solution.py:186
  (87 shorter events, 15.7 us)
Async XLA Ops:
  16.3 6.8 %copy-start.1 = (f32[256,32,128]{2,1,0:T(8,128)}, f32[256,32,128]{2,1,0:T(8,128)S(1)}, u32[]{:S(2)}) copy-start(f32[256,32,128]{2,1,0:T(8,128)S(1)} %add_convert_fusion) | copy-start | bytes 12582916
  23.1 7.1 %copy-start = (f32[2,256,32,128,1,1]{3,2,1,0,5,4:T(8,128)}, f32[2,256,32,128,1,1]{3,2,1,0,5,4:T(8,128)S(1)}, u32[]{:S(2)}) copy-start(f32[2,256,32,128,1,1]{3,2,1,0,5,4:T(8,128)S(1)} %fusion) | copy-start | bytes 25165828
  31.7 51.1 %all-to-all-start.2 = ((f32[1,2,8,8,32,128]{5,3,1,4,0,2:T(8,128)}), f32[1,2,8,8,32,128]{5,3,1,4,0,2:T(8,128)S(1)}, u32[]{:S(2)}, u32[]{:S(2)}) async-start(f32[1,2,8,8,32,128]{5,3,1,4,0,2:T(8,128)} %copy.131), calls=%async_computation.2 | async-start | bytes 4194304 | tf_op jit(solution)/shard_map/all_to_all | solution.py:143
  82.8 1.4 copy-start.6
  84.2 53.3 %all-to-all-start = ((f32[1,2,8,8,32,128]{5,3,1,4,0,2:T(8,128)}), f32[1,2,8,8,32,128]{5,3,1,4,0,2:T(8,128)}, u32[]{:S(2)}, u32[]{:S(2)}) async-start(f32[1,2,8,8,32,128]{5,3,1,4,0,2:T(8,128)} %copy.123), calls=%async_computation | async-start | bytes 4194304 | tf_op jit(solution)/shard_map/all_to_all | solution.py:143
  137.4 52.7 %all-to-all-start.6 = ((f32[1,2,8,8,32,128]{5,3,1,4,0,2:T(8,128)}), f32[1,2,8,8,32,128]{5,3,1,4,0,2:T(8,128)S(1)}, u32[]{:S(2)}, u32[]{:S(2)}) async-start(f32[1,2,8,8,32,128]{5,3,1,4,0,2:T(8,128)} %copy.145), calls=%async_computation.6 | async-start | bytes 4194304 | tf_op jit(solution)/shard_map/all_to_all | solution.py:143
  190.1 53.3 %all-to-all-start.4 = ((f32[1,2,8,8,32,128]{5,3,1,4,0,2:T(8,128)}), f32[1,2,8,8,32,128]{5,3,1,4,0,2:T(8,128)}, u32[]{:S(2)}, u32[]{:S(2)}) async-start(f32[1,2,8,8,32,128]{5,3,1,4,0,2:T(8,128)} %copy.138), calls=%async_computation.4 | async-start | bytes 4194304 | tf_op jit(solution)/shard_map/all_to_all | solution.py:143
  197.8 4.1 copy-start.9
  201.9 4.1 copy-start.17
  201.9 4.1 copy-start.19
  206.0 7.2 %copy-start.5 = (f32[1,2,8,256,256]{4,3,1,2,0:T(8,128)S(1)}, f32[1,2,8,256,256]{4,3,1,2,0:T(8,128)}, u32[]{:S(2)}) copy-start(f32[1,2,8,256,256]{4,3,1,2,0:T(8,128)} %get-tuple-element.96) | copy-start | bytes 12582916
  209.6 3.6 copy-start.4
  213.2 10.2 %copy-start.11 = (f32[1,128,2,256]{3,1,2,0:T(8,128)S(1)}, f32[1,128,2,256]{3,1,2,0:T(8,128)}, u32[]{:S(2)}) copy-start(f32[1,128,2,256]{3,1,2,0:T(8,128)} %get-tuple-element.42) | copy-start | bytes 786436
  213.3 10.2 %copy-start.14 = (f32[1,128,2,256]{3,1,2,0:T(8,128)S(1)}, f32[1,128,2,256]{3,1,2,0:T(8,128)}, u32[]{:S(2)}) copy-start(f32[1,128,2,256]{3,1,2,0:T(8,128)} %get-tuple-element.43) | copy-start | bytes 786436
  243.4 53.4 %all-to-all-start.1 = ((f32[1,2,8,8,32,128]{5,4,1,3,0,2:T(8,128)}), f32[1,2,8,8,32,128]{5,4,1,3,0,2:T(8,128)}, u32[]{:S(2)}, u32[]{:S(2)}) async-start(f32[1,2,8,8,32,128]{5,4,1,3,0,2:T(8,128)} %copy.127), calls=%async_computation.1 | async-start | bytes 4194304 | tf_op jit(solution)/shard_map/all_to_all | solution.py:143
  251.2 8.1 %copy-start.7 = (f32[1,1,8,256,256]{4,3,1,2,0:T(8,128)S(1)}, f32[1,1,8,256,256]{4,3,1,2,0:T(8,128)}, u32[]{:S(2)}) copy-start(f32[1,1,8,256,256]{4,3,1,2,0:T(8,128)} %get-tuple-element.72) | copy-start | bytes 6291460
  251.2 8.1 %copy-start.8 = (f32[1,1,8,256,256]{4,3,1,2,0:T(8,128)S(1)}, f32[1,1,8,256,256]{4,3,1,2,0:T(8,128)}, u32[]{:S(2)}) copy-start(f32[1,1,8,256,256]{4,3,1,2,0:T(8,128)} %get-tuple-element.73) | copy-start | bytes 6291460
  251.2 8.1 %copy-start.12 = (f32[1,128,2,256]{3,1,2,0:T(8,128)S(1)}, f32[1,128,2,256]{3,1,2,0:T(8,128)}, u32[]{:S(2)}) copy-start(f32[1,128,2,256]{3,1,2,0:T(8,128)} %get-tuple-element.42) | copy-start | bytes 786436
  251.2 8.1 %copy-start.15 = (f32[1,128,2,256]{3,1,2,0:T(8,128)S(1)}, f32[1,128,2,256]{3,1,2,0:T(8,128)}, u32[]{:S(2)}) copy-start(f32[1,128,2,256]{3,1,2,0:T(8,128)} %get-tuple-element.43) | copy-start | bytes 786436
  296.8 53.6 %all-to-all-start.3 = ((f32[1,2,8,8,32,128]{5,4,1,3,0,2:T(8,128)}), f32[1,2,8,8,32,128]{5,4,1,3,0,2:T(8,128)}, u32[]{:S(2)}, u32[]{:S(2)}) async-start(f32[1,2,8,8,32,128]{5,4,1,3,0,2:T(8,128)} %copy.135), calls=%async_computation.3 | async-start | bytes 4194304 | tf_op jit(solution)/shard_map/all_to_all | solution.py:143
  304.8 3.5 copy-start.10
  308.3 4.1 copy-start.18
  308.3 4.1 copy-start.20
  312.4 7.2 %copy-start.3 = (f32[1,2,8,256,256]{4,3,1,2,0:T(8,128)S(1)}, f32[1,2,8,256,256]{4,3,1,2,0:T(8,128)}, u32[]{:S(2)}) copy-start(f32[1,2,8,256,256]{4,3,1,2,0:T(8,128)} %get-tuple-element.94) | copy-start | bytes 12582916
  316.0 3.6 copy-start.2
  319.7 10.0 %copy-start.13 = (f32[1,128,2,256]{3,1,2,0:T(8,128)S(1)}, f32[1,128,2,256]{3,1,2,0:T(8,128)}, u32[]{:S(2)}) copy-start(f32[1,128,2,256]{3,1,2,0:T(8,128)} %get-tuple-element.42) | copy-start | bytes 786436
  319.7 10.0 %copy-start.16 = (f32[1,128,2,256]{3,1,2,0:T(8,128)S(1)}, f32[1,128,2,256]{3,1,2,0:T(8,128)}, u32[]{:S(2)}) copy-start(f32[1,128,2,256]{3,1,2,0:T(8,128)} %get-tuple-element.43) | copy-start | bytes 786436
  350.3 52.7 %all-to-all-start.5 = ((f32[1,2,8,8,32,128]{5,4,1,3,0,2:T(8,128)}), f32[1,2,8,8,32,128]{5,4,1,3,0,2:T(8,128)S(1)}, u32[]{:S(2)}, u32[]{:S(2)}) async-start(f32[1,2,8,8,32,128]{5,4,1,3,0,2:T(8,128)} %copy.142), calls=%async_computation.5 | async-start | bytes 4194304 | tf_op jit(solution)/shard_map/all_to_all | solution.py:143
  403.0 53.7 %all-to-all-start.7 = ((f32[1,2,8,8,32,128]{5,4,1,3,0,2:T(8,128)}), f32[1,2,8,8,32,128]{5,4,1,3,0,2:T(8,128)}, u32[]{:S(2)}, u32[]{:S(2)}) async-start(f32[1,2,8,8,32,128]{5,4,1,3,0,2:T(8,128)} %copy.149), calls=%async_computation.7 | async-start | bytes 4194304 | tf_op jit(solution)/shard_map/all_to_all | solution.py:143
where the time goes:
time: 582 us; the launch traced here: 575 us
  waiting for transfers between devices  192 us (33%)
  matrix products  131 us (23%)
  local copies, waits for them, and re-layouts  77.7 us (13%)
  other arithmetic  69.2 us (12%)
  starting transfers between devices  59.5 us (10%)
  blocking collectives  43.2 us (7%)
    all_to_all x8, waiting for transfers between devices, exchange(): lax.all_to_all(values, 'grid', split_axis=2, concat_axis=2, tiled=True)  192 us
    dot_general x24, matrix products, contract(): return jnp.einsum(pattern, table, values, precision=lax.Precision.HIGH)  128 us
    all_to_all x8, starting transfers between devices, exchange(): lax.all_to_all(values, 'grid', split_axis=2, concat_axis=2, tiled=True)  59.5 us
    psum x1, blocking collectives, shards(): total_hist = lax.psum(local_hist, ('traj', 'grid'))  43.2 us
    add x2, other arithmetic, shards(): field_real * evo_real - field_imag * evo_imag + kick[:, 0]  20.2 us
    slice x2, local copies, waits for them, and re-layouts, shards(): out[..., :quarter]  17.1 us
    transpose x8, local copies, waits for them, and re-layouts, contract(): return jnp.einsum(pattern, table, values, precision=lax.Precision.HIGH)  14.1 us
    concatenate x1, other arithmetic, shards(): jnp.concatenate([out[..., :quarter], filler, out[..., quarter:]], axis=-1)  13 us
  transfers between devices with their start and end apart: 8, of which 8 were waited for; matrix products, arithmetic and copies ran while one was open for 30% of the time, Pallas kernels for 0%

commit v1 on v0

--- a/solution.py
+++ b/solution.py
@@ -11,6 +11,12 @@
 noise_amp = 0.1
 trap_strength = 8.0
 max_chunks = 4
+
+
+def gather_and_add(shard, axis):
+    terms = lax.all_gather(shard, axis, axis=0, tiled=False)
+    acc = terms.sum(axis=0)
+    return acc
 
 
 def signed_of(index, count):
@@ -179,7 +185,7 @@
     out = final * kept
     occupation = jnp.sum(out * out, axis=(0, 1))
     local_hist = shell_sums(occupation, modes_x, modes_y, modes_z, 2 * quarter * quarter)
-    total_hist = lax.psum(local_hist, ("traj", "grid"))
+    total_hist = gather_and_add(local_hist, ("traj", "grid"))
     traj_count = psi_modes.shape[0] * lax.axis_size("traj")
     momentum_hist = total_hist * (SHELLS / (traj_count * extent_x * extent_y * extent_z))
     filler = jnp.zeros(out.shape[:-1] + (extent_z - 2 * quarter,), jnp.float32)

time: 582 us -> 583 us (level)
  the two profiles are of different devices: /device:TPU:10 before, /device:TPU:0 now
where the time goes in v1:
time: 583 us; the launch traced here: 576 us
  waiting for transfers between devices  220 us (38%)
  matrix products  132 us (23%)
  local copies, waits for them, and re-layouts  78 us (13%)
  other arithmetic  69 us (12%)
  blocking collectives  39.5 us (7%)
  starting transfers between devices  36.5 us (6%)
    all_to_all x8, waiting for transfers between devices, exchange(): lax.all_to_all(values, 'grid', split_axis=2, concat_axis=2, tiled=True)  220 us
    dot_general x24, matrix products, contract(): return jnp.einsum(pattern, table, values, precision=lax.Precision.HIGH)  128 us
    all_gather x1, blocking collectives, gather_and_add(): terms = lax.all_gather(shard, axis, axis=0, tiled=False)  39.5 us
    all_to_all x8, starting transfers between devices, exchange(): lax.all_to_all(values, 'grid', split_axis=2, concat_axis=2, tiled=True)  36.5 us
    add x2, other arithmetic, shards(): field_real * evo_real - field_imag * evo_imag + kick[:, 0]  20.1 us
    slice x2, local copies, waits for them, and re-layouts, shards(): out[..., :quarter]  17.3 us
    transpose x8, local copies, waits for them, and re-layouts, contract(): return jnp.einsum(pattern, table, values, precision=lax.Precision.HIGH)  14.1 us
    concatenate x1, other arithmetic, shards(): jnp.concatenate([out[..., :quarter], filler, out[..., quarter:]], axis=-1)  13 us
  transfers between devices with their start and end apart: 8, of which 8 were waited for; matrix products, arithmetic and copies ran while one was open for 30% of the time, Pallas kernels for 0%

profile of v1, /device:TPU:0, one launch (start us, length us, event | category | flops | bytes accessed | tf_op | source)
XLA Modules:
  0.0 576.2 jit_solution(5715232873066424755)
XLA Ops:
  0.8 4.9 fusion.186
  5.8 9.4 %slice_bitcast_fusion.1 = (f32[2,256,32,64]{3,2,1,0:T(8,128)S(1)}, f32[2,256,32,64]{3,2,1,0:T(8,128)}) fusion(f32[1,2,256,32,256]{4,3,2,1,0:T(8,128)} %param.3), kind=kLoop, calls=%fused_computation.15 | loop fusion | bytes 16777216 | tf_op jit(solution)/shard_map/concatenate | solution.py:116
  17.5 5.3 fusion
  22.9 7.0 %fusion.104 = f32[1,2,8,8,32,128]{5,3,2,1,4,0:T(8,128)S(1)} fusion(f32[2,256,32,128,1,1]{3,2,1,0,5,4:T(8,128)S(1)} %fusion, f32[2,8,4,8,2,256]{5,3,4,1,0,2:T(8,128)S(1)} %maximum_maximum_fusion), kind=kOutput, calls=%fused_computation.202 | convolution fusion | flops 1610612736 | bytes 10747904 | tf_op jit(solution)/shard_map/dgpcx,tcxyz->tdgpyz/dot_general | solution.py:58
  30.0 1.6 copy.131
  31.5 7.0 %all-to-all-start.2 = ((f32[1,2,8,8,32,128]{5,3,1,4,0,2:T(8,128)}), f32[1,2,8,8,32,128]{5,3,1,4,0,2:T(8,128)S(1)}, u32[]{:S(2)}, u32[]{:S(2)}) async-start(f32[1,2,8,8,32,128]{5,3,1,4,0,2:T(8,128)} %copy.131), calls=%async_computation.2 | async-start | bytes 4194304 | tf_op jit(solution)/shard_map/all_to_all | solution.py:149
  38.5 9.9 %fusion.101 = f32[1,2,8,8,32,128]{5,3,2,1,4,0:T(8,128)S(1)} fusion(f32[2,256,32,128,1,1]{3,2,1,0,5,4:T(8,128)} %copy-done, f32[2,8,4,8,2,256]{5,3,4,1,0,2:T(8,128)S(1)} %maximum_maximum_fusion), kind=kOutput, calls=%fused_computation.201 | convolution fusion | flops 1610612736 | bytes 10747904 | tf_op jit(solution)/shard_map/dgpcx,tcxyz->tdgpyz/dot_general | solution.py:58
  50.0 37.5 %all-to-all-done.2 = f32[1,2,8,8,32,128]{5,3,1,4,0,2:T(8,128)S(1)} async-done(((f32[1,2,8,8,32,128]{5,3,1,4,0,2:T(8,128)}), f32[1,2,8,8,32,128]{5,3,1,4,0,2:T(8,128)S(1)}, u32[]{:S(2)}, u32[]{:S(2)}) %all-to-all-start.2) | async-done | bytes 2097184 | tf_op jit(solution)/shard_map/all_to_all | solution.py:149
  88.9 4.5 all-to-all-start
  93.4 9.9 %fusion.110 = f32[1,2,8,8,32,128]{5,3,2,1,4,0:T(8,128)S(1)} fusion(f32[2,256,32,128,1,1]{3,2,1,0,5,4:T(8,128)} %copy-done, f32[2,8,4,8,2,256]{5,3,4,1,0,2:T(8,128)S(1)} %maximum_maximum_fusion), kind=kOutput, calls=%fused_computation.204 | convolution fusion | flops 1610612736 | bytes 10747904 | tf_op jit(solution)/shard_map/dgpcx,tcxyz->tdgpyz/dot_general | solution.py:58
  105.1 11.6 %fusion.107 = f32[1,2,8,8,32,128]{5,3,2,1,4,0:T(8,128)} fusion(f32[2,256,32,128,1,1]{3,2,1,0,5,4:T(8,128)} %copy-done, f32[2,8,4,8,2,256]{5,3,4,1,0,2:T(8,128)S(1)} %maximum_maximum_fusion), kind=kOutput, calls=%fused_computation.203 | convolution fusion | flops 1610612736 | bytes 10747904 | tf_op jit(solution)/shard_map/dgpcx,tcxyz->tdgpyz/dot_general | solution.py:58
  116.7 25.6 %all-to-all-done = f32[1,2,8,8,32,128]{5,3,1,4,0,2:T(8,128)} async-done(((f32[1,2,8,8,32,128]{5,3,1,4,0,2:T(8,128)}), f32[1,2,8,8,32,128]{5,3,1,4,0,2:T(8,128)}, u32[]{:S(2)}, u32[]{:S(2)}) %all-to-all-start) | async-done | bytes 2097184 | tf_op jit(solution)/shard_map/all_to_all | solution.py:149
  142.2 3.6 all-to-all-start.6
  146.3 3.2 copy.138
  152.5 1.9 fusion.155
  155.6 10.1 %fusion.184 = (f32[1,2,8,256,256]{4,3,2,1,0:T(8,128)}, f32[1,2,8,256,256]{4,3,2,1,0:T(8,128)}, f32[1,2,8,256,256]{4,3,2,1,0:T(8,128)S(1)}, f32[1,2,8,256,256]{4,3,2,1,0:T(8,128)S(1)}) fusion(f32[1,2,32,256,256]{4,3,2,1,0:T(8,128)} %param.4), kind=kLoop, calls=%fused_computation.386 | loop fusion | bytes 33554432 | tf_op jit(solution)/shard_map/slice | solution.py:172
  165.7 4.0 copy_multiply_fusion.2
  169.7 25.1 %all-to-all-done.6 = f32[1,2,8,8,32,128]{5,3,1,4,0,2:T(8,128)S(1)} async-done(((f32[1,2,8,8,32,128]{5,3,1,4,0,2:T(8,128)}), f32[1,2,8,8,32,128]{5,3,1,4,0,2:T(8,128)S(1)}, u32[]{:S(2)}, u32[]{:S(2)}) %all-to-all-start.6) | async-done | bytes 2097184 | tf_op jit(solution)/shard_map/all_to_all | solution.py:149
  194.8 4.3 all-to-all-start.4
  199.2 4.1 fusion.84
  203.3 4.1 fusion.90
  207.4 3.6 convolution_bitcast_fusion.2
  211.0 3.6 convolution_bitcast_fusion.3
  214.7 10.0 %slice_add_fusion.7 = (f32[1,1,8,256,256]{4,3,1,2,0:T(8,128)S(1)}, f32[1,1,8,256,256]{4,3,1,2,0:T(8,128)S(1)}, f32[1,1,8,256,256]{4,3,1,2,0:T(8,128)}, f32[1,1,8,256,256]{4,3,1,2,0:T(8,128)}) fusion(f32[1,2,8,256,256]{4,3,1,2,0:T(8,128)S(1)} %copy-done.5, f32[1,2,8,256,256]{4,3,1,2,0:T(8,128)S(1)} %convolution_bitcast_fusion.3, ...), kind=kLoop, calls=%fused_computation.136 | loop fusion | flops 61865984 | bytes 25183232 | tf_op jit(solution)/shard_map/add | solution.py:175
  224.6 1.9 fusion.13
  226.5 1.9 fusion.113
  228.4 1.6 copy.127
  230.0 18.2 %all-to-all-done.4 = f32[1,2,8,8,32,128]{5,3,1,4,0,2:T(8,128)} async-done(((f32[1,2,8,8,32,128]{5,3,1,4,0,2:T(8,128)}), f32[1,2,8,8,32,128]{5,3,1,4,0,2:T(8,128)}, u32[]{:S(2)}, u32[]{:S(2)}) %all-to-all-start.4) | async-done | bytes 2097184 | tf_op jit(solution)/shard_map/all_to_all | solution.py:149
  248.2 4.3 all-to-all-start.1
  252.6 8.0 %copy_multiply_fusion = (f32[1,2,8,256,256]{4,3,1,2,0:T(8,128)}, f32[1,2,8,256,256]{4,3,1,2,0:T(8,128)}) fusion(f32[1,2,8,256,256]{4,3,2,1,0:T(8,128)} %get-tuple-element.22, f32[1,2,8,256,256]{4,3,2,1,0:T(8,128)} %get-tuple-element.23), kind=kLoop, calls=%fused_computation.41 | loop fusion | flops 2097152 | bytes 16777216 | tf_op jit(solution)/shard_map/mul | solution.py:172
  260.6 1.9 fusion.16
  262.5 1.9 fusion.116
  264.4 1.6 copy.135
  266.0 35.6 %all-to-all-done.1 = f32[1,2,8,8,32,128]{5,4,1,3,0,2:T(8,128)} async-done(((f32[1,2,8,8,32,128]{5,4,1,3,0,2:T(8,128)}), f32[1,2,8,8,32,128]{5,4,1,3,0,2:T(8,128)}, u32[]{:S(2)}, u32[]{:S(2)}) %all-to-all-start.1) | async-done | bytes 2097184 | tf_op jit(solution)/shard_map/all_to_all | solution.py:149
  301.6 4.6 all-to-all-start.3
  306.2 3.5 fusion.72
  309.7 4.1 fusion.78
  313.8 3.6 convolution_bitcast_fusion
  317.4 3.6 convolution_bitcast_fusion.1
  321.0 10.2 %slice_add_fusion.1 = (f32[1,1,8,256,256]{4,3,1,2,0:T(8,128)}, f32[1,1,8,256,256]{4,3,1,2,0:T(8,128)}, f32[1,1,8,256,256]{4,3,1,2,0:T(8,128)S(1)}, f32[1,1,8,256,256]{4,3,1,2,0:T(8,128)S(1)}) fusion(f32[1,2,8,256,256]{4,3,1,2,0:T(8,128)S(1)} %copy-done.2, f32[1,2,8,256,256]{4,3,1,2,0:T(8,128)S(1)} %convolution_bitcast_fusion, ...), kind=kLoop, calls=%fused_computation.130 | loop fusion | flops 61865984 | bytes 25183232 | tf_op jit(solution)/shard_map/add | solution.py:175
  331.2 1.9 fusion.19
  333.1 1.9 fusion.119
  336.5 18.7 %all-to-all-done.3 = f32[1,2,8,8,32,128]{5,4,1,3,0,2:T(8,128)} async-done(((f32[1,2,8,8,32,128]{5,4,1,3,0,2:T(8,128)}), f32[1,2,8,8,32,128]{5,4,1,3,0,2:T(8,128)}, u32[]{:S(2)}, u32[]{:S(2)}) %all-to-all-start.3) | async-done | bytes 2097184 | tf_op jit(solution)/shard_map/all_to_all | solution.py:149
  355.2 3.6 all-to-all-start.5
  358.8 3.7 fusion.22
  362.5 1.9 fusion.122
  364.4 1.6 copy.149
  366.0 41.8 %all-to-all-done.5 = f32[1,2,8,8,32,128]{5,4,1,3,0,2:T(8,128)S(1)} async-done(((f32[1,2,8,8,32,128]{5,4,1,3,0,2:T(8,128)}), f32[1,2,8,8,32,128]{5,4,1,3,0,2:T(8,128)S(1)}, u32[]{:S(2)}, u32[]{:S(2)}) %all-to-all-start.5) | async-done | bytes 2097184 | tf_op jit(solution)/shard_map/all_to_all | solution.py:149
  407.8 4.5 all-to-all-start.7
  412.4 5.3 copy.151
  419.3 8.8 %fusion.86 = f32[32,128,2,256,1,1]{3,1,5,4,2,0:T(8,128)} fusion(f32[1,2,8,8,32,128]{5,4,1,3,0,2:T(8,128)} %all-to-all-done.1, f32[2,256,2,8,4,8]{1,3,5,2,0,4:T(8,128)S(1)} %maximum_maximum_fusion.1), kind=kOutput, calls=%fused_computation.158 | convolution fusion | flops 1610612736 | bytes 10747904 | tf_op jit(solution)/shard_map/ekdsp,tdspyz->tekyz/dot_general | solution.py:58
  428.1 8.8 %fusion.80 = f32[32,128,2,256,1,1]{3,1,5,4,2,0:T(8,128)} fusion(f32[1,2,8,8,32,128]{5,4,1,3,0,2:T(8,128)} %all-to-all-done.3, f32[2,256,2,8,4,8]{1,3,5,2,0,4:T(8,128)S(1)} %maximum_maximum_fusion.1), kind=kOutput, calls=%fused_computation.152 | convolution fusion | flops 1610612736 | bytes 10747904 | tf_op jit(solution)/shard_map/ekdsp,tdspyz->tekyz/dot_general | solution.py:58
  436.9 6.8 %fusion.74 = f32[32,128,2,256,1,1]{3,1,5,4,2,0:T(8,128)} fusion(f32[1,2,8,8,32,128]{5,4,1,3,0,2:T(8,128)S(1)} %all-to-all-done.5, f32[2,256,2,8,4,8]{1,3,5,2,0,4:T(8,128)S(1)} %maximum_maximum_fusion.1), kind=kOutput, calls=%fused_computation.146 | convolution fusion | flops 1610612736 | bytes 10747904 | tf_op jit(solution)/shard_map/ekdsp,tdspyz->tekyz/dot_general | solution.py:58
  443.8 17.6 %all-to-all-done.7 = f32[1,2,8,8,32,128]{5,4,1,3,0,2:T(8,128)} async-done(((f32[1,2,8,8,32,128]{5,4,1,3,0,2:T(8,128)}), f32[1,2,8,8,32,128]{5,4,1,3,0,2:T(8,128)}, u32[]{:S(2)}, u32[]{:S(2)}) %all-to-all-start.7) | async-done | bytes 2097184 | tf_op jit(solution)/shard_map/all_to_all | solution.py:149
  461.3 18.4 %multiply_reduce_fusion = (f32[256,32,128]{0,2,1:T(8,128)}, f32[1,2,256,32,128]{2,4,1,3,0:T(8,128)}) fusion(f32[256,32,128]{0,2,1:T(8,128)} %copy.151, f32[2,256,2,8,4,8]{1,3,5,2,0,4:T(8,128)S(1)} %maximum_maximum_fusion.1, f32[1,2,8,8,32,128]{5,4,1,3,0,2:T(8,128)} %all-to-all-done.7, f32[32,128,2,256,1,1]{3,1,5,4,2,0:T(8,128)} %fusion.74, ...), kind=kOutput, calls=%fused_computation.13 | convolution fusion | flops 1622147072 | bytes 44302336 | tf_op jit(solution)/shard_map/ekdsp,tdspyz->tekyz/dot_general | solution.py:58
  479.7 5.5 copy.154
  485.2 5.9 %bitcast_select_fusion.1 = (f32[8192,128]{1,0:T(8,128)S(1)}, f32[8192,128]{1,0:T(8,128)S(1)}) fusion(f32[256,32,128]{2,1,0:T(8,128)} %copy.154, s32[128]{0:T(128)S(1)} %and_select_fusion, s32[8192]{0:T(1024)S(1)} %get-tuple-element.47), kind=kLoop, calls=%fused_computation.46 | loop fusion | flops 4194304 | bytes 12616192 | tf_op jit(solution)/shard_map/jit(_where)/select_n | solution.py:91
  491.1 3.4 fusion.1
  494.5 1.9 select_reduce_fusion
  496.4 39.5 %all-gather.1 = f32[32,1,128]{2,1,0:T(1,128)S(1)} all-gather(f32[1,1,128]{2,1,0:T(1,128)S(1)} %bitcast.371), channel_id=2, replica_groups=mesh['traj'=4,'grid'=8] {'traj','grid'}, dimensions={0}, use_global_device_ids=true | all-gather | bytes 16896 | tf_op jit(solution)/shard_map/all_gather | solution.py:17
  536.5 7.8 %fusion.185 = (f32[1,2,256,32,64]{2,4,1,3,0:T(8,128)}, f32[1,2,256,32,64]{2,4,1,3,0:T(8,128)}) fusion(f32[1,2,256,32,128]{2,4,1,3,0:T(8,128)} %get-tuple-element.89), kind=kLoop, calls=%fused_computation.387 | loop fusion | bytes 16777216 | tf_op jit(solution)/shard_map/slice | solution.py:192
  544.3 9.5 %copy.152 = f32[1,2,256,32,64]{4,3,2,1,0:T(8,128)} copy(f32[1,2,256,32,64]{2,4,1,3,0:T(8,128)} %get-tuple-element.36) | data formatting | bytes 8388608 | tf_op jit(solution)/shard_map/slice | solution.py:192
  553.8 9.2 %copy.153 = f32[1,2,256,32,64]{4,3,2,1,0:T(8,128)} copy(f32[1,2,256,32,64]{2,4,1,3,0:T(8,128)} %get-tuple-element.37) | data formatting | bytes 8388608 | tf_op jit(solution)/shard_map/slice | solution.py:192
  563.0 13.0 %pad_maximum_fusion = f32[1,2,256,32,256]{4,3,2,1,0:T(8,128)} fusion(f32[1,2,256,32,64]{4,3,2,1,0:T(8,128)} %copy.153, f32[1,2,256,32,64]{4,3,2,1,0:T(8,128)} %copy.152, f32[256]{0:T(256)S(1)} %pad.5.clone), kind=kLoop, calls=%fused_computation | loop fusion | flops 8388608 | bytes 25166848 | tf_op jit(solution)/shard_map/concatenate | solution.py:192
  (88 shorter events, 15.7 us)
Async XLA Ops:
  16.3 6.6 %copy-start.1 = (f32[256,32,128]{2,1,0:T(8,128)}, f32[256,32,128]{2,1,0:T(8,128)S(1)}, u32[]{:S(2)}) copy-start(f32[256,32,128]{2,1,0:T(8,128)S(1)} %add_convert_fusion) | copy-start | bytes 12582916
  22.9 7.0 %copy-start = (f32[2,256,32,128,1,1]{3,2,1,0,5,4:T(8,128)}, f32[2,256,32,128,1,1]{3,2,1,0,5,4:T(8,128)S(1)}, u32[]{:S(2)}) copy-start(f32[2,256,32,128,1,1]{3,2,1,0,5,4:T(8,128)S(1)} %fusion) | copy-start | bytes 25165828
  31.5 56.0 %all-to-all-start.2 = ((f32[1,2,8,8,32,128]{5,3,1,4,0,2:T(8,128)}), f32[1,2,8,8,32,128]{5,3,1,4,0,2:T(8,128)S(1)}, u32[]{:S(2)}, u32[]{:S(2)}) async-start(f32[1,2,8,8,32,128]{5,3,1,4,0,2:T(8,128)} %copy.131), calls=%async_computation.2 | async-start | bytes 4194304 | tf_op jit(solution)/shard_map/all_to_all | solution.py:149
  87.5 1.4 copy-start.6
  88.9 53.4 %all-to-all-start = ((f32[1,2,8,8,32,128]{5,3,1,4,0,2:T(8,128)}), f32[1,2,8,8,32,128]{5,3,1,4,0,2:T(8,128)}, u32[]{:S(2)}, u32[]{:S(2)}) async-start(f32[1,2,8,8,32,128]{5,3,1,4,0,2:T(8,128)} %copy.123), calls=%async_computation | async-start | bytes 4194304 | tf_op jit(solution)/shard_map/all_to_all | solution.py:149
  142.2 52.6 %all-to-all-start.6 = ((f32[1,2,8,8,32,128]{5,3,1,4,0,2:T(8,128)}), f32[1,2,8,8,32,128]{5,3,1,4,0,2:T(8,128)S(1)}, u32[]{:S(2)}, u32[]{:S(2)}) async-start(f32[1,2,8,8,32,128]{5,3,1,4,0,2:T(8,128)} %copy.145), calls=%async_computation.6 | async-start | bytes 4194304 | tf_op jit(solution)/shard_map/all_to_all | solution.py:149
  194.8 53.4 %all-to-all-start.4 = ((f32[1,2,8,8,32,128]{5,3,1,4,0,2:T(8,128)}), f32[1,2,8,8,32,128]{5,3,1,4,0,2:T(8,128)}, u32[]{:S(2)}, u32[]{:S(2)}) async-start(f32[1,2,8,8,32,128]{5,3,1,4,0,2:T(8,128)} %copy.138), calls=%async_computation.4 | async-start | bytes 4194304 | tf_op jit(solution)/shard_map/all_to_all | solution.py:149
  199.2 4.1 copy-start.9
  203.3 4.1 copy-start.17
  203.3 4.1 copy-start.19
  207.4 7.2 %copy-start.5 = (f32[1,2,8,256,256]{4,3,1,2,0:T(8,128)S(1)}, f32[1,2,8,256,256]{4,3,1,2,0:T(8,128)}, u32[]{:S(2)}) copy-start(f32[1,2,8,256,256]{4,3,1,2,0:T(8,128)} %get-tuple-element.96) | copy-start | bytes 12582916
  211.0 3.6 copy-start.4
  214.6 10.0 %copy-start.11 = (f32[1,128,2,256]{3,1,2,0:T(8,128)S(1)}, f32[1,128,2,256]{3,1,2,0:T(8,128)}, u32[]{:S(2)}) copy-start(f32[1,128,2,256]{3,1,2,0:T(8,128)} %get-tuple-element.42) | copy-start | bytes 786436
  214.6 10.0 %copy-start.14 = (f32[1,128,2,256]{3,1,2,0:T(8,128)S(1)}, f32[1,128,2,256]{3,1,2,0:T(8,128)}, u32[]{:S(2)}) copy-start(f32[1,128,2,256]{3,1,2,0:T(8,128)} %get-tuple-element.43) | copy-start | bytes 786436
  248.2 53.4 %all-to-all-start.1 = ((f32[1,2,8,8,32,128]{5,4,1,3,0,2:T(8,128)}), f32[1,2,8,8,32,128]{5,4,1,3,0,2:T(8,128)}, u32[]{:S(2)}, u32[]{:S(2)}) async-start(f32[1,2,8,8,32,128]{5,4,1,3,0,2:T(8,128)} %copy.127), calls=%async_computation.1 | async-start | bytes 4194304 | tf_op jit(solution)/shard_map/all_to_all | solution.py:149
  252.5 8.1 %copy-start.7 = (f32[1,1,8,256,256]{4,3,1,2,0:T(8,128)S(1)}, f32[1,1,8,256,256]{4,3,1,2,0:T(8,128)}, u32[]{:S(2)}) copy-start(f32[1,1,8,256,256]{4,3,1,2,0:T(8,128)} %get-tuple-element.72) | copy-start | bytes 6291460
  252.6 8.1 %copy-start.8 = (f32[1,1,8,256,256]{4,3,1,2,0:T(8,128)S(1)}, f32[1,1,8,256,256]{4,3,1,2,0:T(8,128)}, u32[]{:S(2)}) copy-start(f32[1,1,8,256,256]{4,3,1,2,0:T(8,128)} %get-tuple-element.73) | copy-start | bytes 6291460
  252.6 8.1 %copy-start.12 = (f32[1,128,2,256]{3,1,2,0:T(8,128)S(1)}, f32[1,128,2,256]{3,1,2,0:T(8,128)}, u32[]{:S(2)}) copy-start(f32[1,128,2,256]{3,1,2,0:T(8,128)} %get-tuple-element.42) | copy-start | bytes 786436
  252.6 8.1 %copy-start.15 = (f32[1,128,2,256]{3,1,2,0:T(8,128)S(1)}, f32[1,128,2,256]{3,1,2,0:T(8,128)}, u32[]{:S(2)}) copy-start(f32[1,128,2,256]{3,1,2,0:T(8,128)} %get-tuple-element.43) | copy-start | bytes 786436
  301.6 53.6 %all-to-all-start.3 = ((f32[1,2,8,8,32,128]{5,4,1,3,0,2:T(8,128)}), f32[1,2,8,8,32,128]{5,4,1,3,0,2:T(8,128)}, u32[]{:S(2)}, u32[]{:S(2)}) async-start(f32[1,2,8,8,32,128]{5,4,1,3,0,2:T(8,128)} %copy.135), calls=%async_computation.3 | async-start | bytes 4194304 | tf_op jit(solution)/shard_map/all_to_all | solution.py:149
  306.2 3.5 copy-start.10
  309.7 4.1 copy-start.18
  309.7 4.1 copy-start.20
  313.8 7.2 %copy-start.3 = (f32[1,2,8,256,256]{4,3,1,2,0:T(8,128)S(1)}, f32[1,2,8,256,256]{4,3,1,2,0:T(8,128)}, u32[]{:S(2)}) copy-start(f32[1,2,8,256,256]{4,3,1,2,0:T(8,128)} %get-tuple-element.94) | copy-start | bytes 12582916
  317.4 3.6 copy-start.2
  321.0 10.2 %copy-start.13 = (f32[1,128,2,256]{3,1,2,0:T(8,128)S(1)}, f32[1,128,2,256]{3,1,2,0:T(8,128)}, u32[]{:S(2)}) copy-start(f32[1,128,2,256]{3,1,2,0:T(8,128)} %get-tuple-element.42) | copy-start | bytes 786436
  321.0 10.2 %copy-start.16 = (f32[1,128,2,256]{3,1,2,0:T(8,128)S(1)}, f32[1,128,2,256]{3,1,2,0:T(8,128)}, u32[]{:S(2)}) copy-start(f32[1,128,2,256]{3,1,2,0:T(8,128)} %get-tuple-element.43) | copy-start | bytes 786436
  355.2 52.6 %all-to-all-start.5 = ((f32[1,2,8,8,32,128]{5,4,1,3,0,2:T(8,128)}), f32[1,2,8,8,32,128]{5,4,1,3,0,2:T(8,128)S(1)}, u32[]{:S(2)}, u32[]{:S(2)}) async-start(f32[1,2,8,8,32,128]{5,4,1,3,0,2:T(8,128)} %copy.142), calls=%async_computation.5 | async-start | bytes 4194304 | tf_op jit(solution)/shard_map/all_to_all | solution.py:149
  407.8 53.6 %all-to-all-start.7 = ((f32[1,2,8,8,32,128]{5,4,1,3,0,2:T(8,128)}), f32[1,2,8,8,32,128]{5,4,1,3,0,2:T(8,128)}, u32[]{:S(2)}, u32[]{:S(2)}) async-start(f32[1,2,8,8,32,128]{5,4,1,3,0,2:T(8,128)} %copy.149), calls=%async_computation.7 | async-start | bytes 4194304 | tf_op jit(solution)/shard_map/all_to_all | solution.py:149
